TPU v7x, 32 devices: a 4x4x1 block of a 4x4x8 slice. The times are simulated.
32 devices in a mesh: rep: 1 (over z), data: 32 (over y, x, core).
Axes of the slice: x: 4, y: 4, z: 1, core: 2. Of those that a mesh axis runs over, the one named last changes fastest.
The devices are a block of a 4x4x8 slice.
Arguments:
- x: bfloat16 [8192, 4096], P(('rep', 'data'))
- adapter_id: int32 [8192], P(('rep', 'data'))
- dout: bfloat16 [8192, 4096], P(('rep', 'data'))
- w_gate: bfloat16 [4096, 14336], replicated
- w_up: bfloat16 [4096, 14336], replicated
- w_down: bfloat16 [14336, 4096], replicated
- a_gate: bfloat16 [64, 4096, 32], P('data')
- b_gate: bfloat16 [64, 32, 14336], P('data')
- a_up: bfloat16 [64, 4096, 32], P('data')
- b_up: bfloat16 [64, 32, 14336], P('data')
- a_down: bfloat16 [64, 14336, 32], P('data')
- b_down: bfloat16 [64, 32, 4096], P('data')
Outputs:
- output 1: bfloat16 [8192, 4096], P(('rep', 'data'))
- output 2: bfloat16 [8192, 4096], P(('rep', 'data'))
- output 3: float32 [64, 4096, 32], P(('rep', 'data'))
- output 4: float32 [64, 32, 14336], P(('rep', 'data'))
- output 5: float32 [64, 4096, 32], P(('rep', 'data'))
- output 6: float32 [64, 32, 14336], P(('rep', 'data'))
- output 7: float32 [64, 14336, 32], P(('rep', 'data'))
- output 8: float32 [64, 32, 4096], P(('rep', 'data'))
All inputs are finite; a program needn't handle non-finite values.
Results may differ from a plain program's by a relative error of at most 0.00138.
Values are sent between devices in bfloat16 or wider.
A program may use at most 768 MiB of HBM per device.

v0:
```python
import jax
import jax.numpy as jnp
from jax import lax
from jax.sharding import PartitionSpec as P

value_a10 = 32


def grouped_rows(in_rows, weight_set, group_sizes, contract_dim):
    dim_numbers = lax.RaggedDotDimensionNumbers(
        dot_dimension_numbers=(([1], [contract_dim]), ([], [])),
        lhs_ragged_dimensions=[0],
        rhs_group_dimensions=[0],
    )
    return lax.ragged_dot_general(in_rows, weight_set, group_sizes, dim_numbers, preferred_element_type=jnp.float32)


def grouped_outer(left_rows, right_rows, group_sizes):
    dim_numbers = lax.RaggedDotDimensionNumbers(
        dot_dimension_numbers=(([0], [0]), ([], [])),
        lhs_ragged_dimensions=[0],
        rhs_group_dimensions=[],
    )
    return lax.ragged_dot_general(left_rows, right_rows, group_sizes, dim_numbers, preferred_element_type=jnp.float32)


def contract_last(left_rows, weight):
    return lax.dot_general(left_rows, weight, (((1,), (1,)), ((), ())), preferred_element_type=jnp.float32)


def solution(mesh):
    group_size = mesh.shape['data']
    tok_spec = P(('rep', 'data'), None)
    id_spec = P(('rep', 'data'))
    full_spec = P(None, None)
    own_spec = P('data', None, None)
    grad_spec = P(('rep', 'data'), None, None)

    def device_fn(x_loc, ids_loc, dy_loc, w_gate, w_up, w_down, a_gate, b_gate, a_up, b_up, a_down, b_down):
        tokens = x_loc.shape[0]
        n_local = a_gate.shape[0]
        array_b10 = value_a10 / a_gate.shape[2]
        capacity = ((3 * tokens + 8 * group_size - 1) // (8 * group_size)) * 8
        owner_dev = ids_loc // n_local
        by_owner = jnp.argsort(owner_dev, stable=True)
        position = jnp.argsort(by_owner, stable=True)
        counts = jnp.bincount(owner_dev, length=group_size)
        starts = jnp.cumsum(counts) - counts
        dest_slot = owner_dev * capacity + position - starts[owner_dev]
        slot_token = jnp.full((group_size * capacity,), tokens, jnp.int32).at[dest_slot].set(jnp.arange(tokens, dtype=jnp.int32))

        def pack_rows(in_rows):
            return jnp.take(in_rows, slot_token, axis=0, mode='fill', fill_value=0)

        arrived_ids = lax.all_to_all(pack_rows(ids_loc % n_local), 'data', 0, 0, tiled=True)
        sort_order = jnp.argsort(arrived_ids, stable=True)
        restore = jnp.argsort(sort_order, stable=True)
        group_sizes = jnp.bincount(arrived_ids, length=n_local).astype(jnp.int32)

        def to_owner(in_rows):
            arrived = lax.all_to_all(pack_rows(in_rows), 'data', 0, 0, tiled=True)
            return jnp.take(arrived, sort_order, axis=0)

        def to_source(owner_rows):
            returned = lax.all_to_all(jnp.take(owner_rows, restore, axis=0), 'data', 0, 0, tiled=True)
            return jnp.take(returned, dest_slot, axis=0)

        x_own = to_owner(x_loc)
        p_gate = grouped_rows(x_own, a_gate, group_sizes, 1).astype(jnp.bfloat16)
        p_up = grouped_rows(x_own, a_up, group_sizes, 1).astype(jnp.bfloat16)
        e_gate = to_source((array_b10 * grouped_rows(p_gate, b_gate, group_sizes, 1)).astype(jnp.bfloat16))
        e_up = to_source((array_b10 * grouped_rows(p_up, b_up, group_sizes, 1)).astype(jnp.bfloat16))
        gate_pre = jnp.dot(x_loc, w_gate, preferred_element_type=jnp.float32) + e_gate.astype(jnp.float32)
        up_pre = jnp.dot(x_loc, w_up, preferred_element_type=jnp.float32) + e_up.astype(jnp.float32)
        gate_sig = jax.nn.sigmoid(gate_pre)
        gate_act = gate_pre * gate_sig
        hidden = (gate_act * up_pre).astype(jnp.bfloat16)
        h_own = to_owner(hidden)
        p_down = grouped_rows(h_own, a_down, group_sizes, 1).astype(jnp.bfloat16)
        e_down = to_source((array_b10 * grouped_rows(p_down, b_down, group_sizes, 1)).astype(jnp.bfloat16))
        out_loc = (x_loc.astype(jnp.float32) + jnp.dot(hidden, w_down, preferred_element_type=jnp.float32) + e_down.astype(jnp.float32)).astype(jnp.bfloat16)
        dy_own = to_owner(dy_loc)
        q_down = (array_b10 * grouped_rows(dy_own, b_down, group_sizes, 2)).astype(jnp.bfloat16)
        value_a7 = to_source(grouped_rows(q_down, a_down, group_sizes, 2).astype(jnp.bfloat16))
        grad_b_down = array_b10 * grouped_outer(p_down, dy_own, group_sizes)
        grad_a_down = grouped_outer(h_own, q_down, group_sizes)
        d_hidden = contract_last(dy_loc, w_down) + value_a7.astype(jnp.float32)
        d_gate = (d_hidden * up_pre * gate_sig * (1.0 + gate_pre * (1.0 - gate_sig))).astype(jnp.bfloat16)
        d_up = (d_hidden * gate_act).astype(jnp.bfloat16)
        dg_own = to_owner(d_gate)
        du_own = to_owner(d_up)
        q_gate = (array_b10 * grouped_rows(dg_own, b_gate, group_sizes, 2)).astype(jnp.bfloat16)
        q_up = (array_b10 * grouped_rows(du_own, b_up, group_sizes, 2)).astype(jnp.bfloat16)
        array_b7 = to_source((grouped_rows(q_gate, a_gate, group_sizes, 2) + grouped_rows(q_up, a_up, group_sizes, 2)).astype(jnp.bfloat16))
        grad_a_gate = grouped_outer(x_own, q_gate, group_sizes)
        grad_b_gate = array_b10 * grouped_outer(p_gate, dg_own, group_sizes)
        grad_a_up = grouped_outer(x_own, q_up, group_sizes)
        grad_b_up = array_b10 * grouped_outer(p_up, du_own, group_sizes)
        dx_loc = (dy_loc.astype(jnp.float32) + contract_last(d_gate, w_gate) + contract_last(d_up, w_up) + array_b7.astype(jnp.float32)).astype(jnp.bfloat16)
        return out_loc, dx_loc, grad_a_gate, grad_b_gate, grad_a_up, grad_b_up, grad_a_down, grad_b_down

    return jax.shard_map(
        device_fn,
        mesh=mesh,
        in_specs=(tok_spec, id_spec, tok_spec, full_spec, full_spec, full_spec, own_spec, own_spec, own_spec, own_spec, own_spec, own_spec),
        out_specs=(tok_spec, tok_spec, grad_spec, grad_spec, grad_spec, grad_spec, grad_spec, grad_spec),
        check_vma=False,
    )
```

profile of v0, /device:TPU:97, one launch (start us, length us, event | category | flops | bytes accessed | tf_op | source)
XLA Modules:
  0.0 3307.1 jit_solution(7149859911037472616)
XLA Ops:
  79.2 83.8 %all_to_all.129 = bf16[32,24,4096]{2,1,0:T(8,128)(2,1)} all-to-all(bf16[32,24,4096]{2,1,0:T(8,128)(2,1)} %bitcast.93), channel_id=1, replica_groups=mesh['rep'=1,'data'=32] {'data'}, dimensions={0} | all-to-all | bytes 12582912 | tf_op jit(solution)/shard_map/all_to_all | solution.py:61
  392.8 57.5 %gather_fusion.3 = bf16[768,14336]{1,0:T(8,128)(2,1)} fusion(bf16[768,14336]{1,0:T(8,128)(2,1)} %convert_element_type.71, s32[1024]{0:T(1024)S(1)} %pad_clamp_fusion.1), kind=kCustom, calls=%fused_computation.2.clone | custom fusion | bytes 44043264 | tf_op jit(solution)/shard_map/jit(_take)/gather | solution.py:65
  450.4 57.7 %gather_fusion.5 = bf16[768,14336]{1,0:T(8,128)(2,1)} fusion(bf16[768,14336]{1,0:T(8,128)(2,1)} %convert_element_type.74, s32[1024]{0:T(1024)S(1)} %pad_clamp_fusion.1), kind=kCustom, calls=%fused_computation.10.clone | custom fusion | bytes 44043264 | tf_op jit(solution)/shard_map/jit(_take)/gather | solution.py:65
  568.5 57.7 %gather_fusion.13 = bf16[768,14336]{1,0:T(8,128)(2,1)} fusion(bf16[768,14336]{1,0:T(8,128)(2,1)} %convert_element_type.83, s32[1024]{0:T(1024)S(1)} %pad_clamp_fusion.1), kind=kCustom, calls=%fused_computation.12.clone | custom fusion | bytes 44043264 | tf_op jit(solution)/shard_map/jit(_take)/gather | solution.py:65
  626.2 42.1 %broadcast_select_fusion.6 = (bf16[768,14336]{1,0:T(8,128)(2,1)}, bf16[768,14336]{1,0:T(8,128)(2,1)}, bf16[768,14336]{1,0:T(8,128)(2,1)}) fusion(bf16[768,14336]{1,0:T(8,128)(2,1)} %gather_fusion.13, pred[768]{0:T(1024)(128)(4,1)S(1)} %copy-done.18, bf16[768,14336]{1,0:T(8,128)(2,1)} %gather_fusion.5, bf16[768,14336]{1,0:T(8,128)(2,1)} %gather_fusion.3), kind=kLoop, calls=%fused_computation.30 | loop fusion | flops 33030144 | bytes 132121344 | tf_op jit(solution)/shard_map/jit(_take)/select_n | solution.py:65
  668.4 267.6 %all_to_all.130 = bf16[32,24,14336]{2,1,0:T(8,128)(2,1)} all-to-all(bf16[32,24,14336]{2,1,0:T(8,128)(2,1)} %bitcast.87), channel_id=1, replica_groups=mesh['rep'=1,'data'=32] {'data'}, dimensions={0} | all-to-all | bytes 44040192 | tf_op jit(solution)/shard_map/all_to_all | solution.py:65
  936.0 269.6 %all_to_all.131 = bf16[32,24,14336]{2,1,0:T(8,128)(2,1)} all-to-all(bf16[32,24,14336]{2,1,0:T(8,128)(2,1)S(1)} %bitcast.85), channel_id=1, replica_groups=mesh['rep'=1,'data'=32] {'data'}, dimensions={0} | all-to-all | bytes 44040192 | tf_op jit(solution)/shard_map/all_to_all | solution.py:65
  1259.0 231.2 %all-to-all-done.7 = bf16[32,24,14336]{2,1,0:T(8,128)(2,1)} async-done(((bf16[32,24,14336]{2,1,0:T(8,128)(2,1)}), bf16[32,24,14336]{2,1,0:T(8,128)(2,1)}, u32[]{:S(2)}, u32[]{:S(2)}) %all-to-all-start.7) | async-done | bytes 22020128 | tf_op jit(solution)/shard_map/all_to_all | solution.py:65
  1510.1 50.6 %convolution_add_fusion.1 = f32[256,14336]{1,0:T(8,128)} fusion(bf16[256,4096]{1,0:T(8,128)(2,1)S(1)} %copy-done.3, bf16[4096,14336]{1,0:T(8,128)(2,1)} %param.28, bf16[256,14336]{1,0:T(8,128)(2,1)} %gather_fusion.6, pred[256]{0:T(512)(128)(4,1)S(1)} %copy-done.26), kind=kOutput, calls=%fused_computation.34 | convolution fusion | flops 30075781120 | bytes 141558016 | tf_op jit(solution)/shard_map/dot_general | solution.py:74
  1560.7 49.8 %convolution_add_fusion.2 = f32[256,14336]{1,0:T(8,128)} fusion(bf16[256,4096]{1,0:T(8,128)(2,1)} %param.24, bf16[4096,14336]{1,0:T(8,128)(2,1)} %param.27, bf16[256,14336]{1,0:T(8,128)(2,1)} %gather_fusion.4, pred[256]{0:T(512)(128)(4,1)S(1)} %copy-done.26), kind=kOutput, calls=%fused_computation.35 | convolution fusion | flops 30075781120 | bytes 141558016 | tf_op jit(solution)/shard_map/dot_general | solution.py:73
  1610.5 62.9 %multiply_convert_fusion = (bf16[256,14336]{1,0:T(8,128)(2,1)}, bf16[256,14336]{1,0:T(8,128)(2,1)}, bf16[256,14336]{1,0:T(8,128)(2,1)}) fusion(f32[256,14336]{1,0:T(8,128)} %convolution_add_fusion.2, f32[256,14336]{1,0:T(8,128)} %convolution_add_fusion.1, bf16[256,14336]{1,0:T(8,128)(2,1)} %gather_fusion.14, pred[256]{0:T(512)(128)(4,1)S(1)} %copy-done.26, ...), kind=kOutput, calls=%fused_computation.36 | convolution fusion | flops 30130831360 | bytes 178258176 | tf_op jit(solution)/shard_map/dot_general | solution.py:28
  1673.4 41.4 %gather_fusion.7 = bf16[768,14336]{1,0:T(8,128)(2,1)} fusion(bf16[256,14336]{1,0:T(8,128)(2,1)} %get-tuple-element.128, s32[1024]{0:T(1024)S(1)} %copy-done.11), kind=kCustom, calls=%fused_computation.4.clone | custom fusion | bytes 44043264 | tf_op jit(solution)/shard_map/jit(_take)/gather | solution.py:53
  1797.1 43.7 %broadcast_select_fusion.3 = (bf16[768,14336]{1,0:T(8,128)(2,1)}, bf16[768,14336]{1,0:T(8,128)(2,1)}, bf16[768,14336]{1,0:T(8,128)(2,1)}) fusion(bf16[768,14336]{1,0:T(8,128)(2,1)} %gather_fusion.17, pred[768]{0:T(1024)(128)(4,1)S(1)} %copy-done.23, bf16[768,14336]{1,0:T(8,128)(2,1)} %gather_fusion.15, bf16[768,14336]{1,0:T(8,128)(2,1)} %gather_fusion.7), kind=kLoop, calls=%fused_computation.27 | loop fusion | flops 33030144 | bytes 132121344 | tf_op jit(solution)/shard_map/jit(_take)/select_n | solution.py:53
  1840.9 300.4 %all_to_all.132 = bf16[32,24,14336]{2,1,0:T(8,128)(2,1)} all-to-all(bf16[32,24,14336]{2,1,0:T(8,128)(2,1)} %bitcast.86), channel_id=1, replica_groups=mesh['rep'=1,'data'=32] {'data'}, dimensions={0} | all-to-all | bytes 44040192 | tf_op jit(solution)/shard_map/all_to_all | solution.py:61
  2141.4 263.6 %all_to_all.133 = bf16[32,24,14336]{2,1,0:T(8,128)(2,1)} all-to-all(bf16[32,24,14336]{2,1,0:T(8,128)(2,1)S(1)} %bitcast.82), channel_id=1, replica_groups=mesh['rep'=1,'data'=32] {'data'}, dimensions={0} | all-to-all | bytes 44040192 | tf_op jit(solution)/shard_map/all_to_all | solution.py:61
  2435.5 57.3 %gather_fusion.8 = bf16[768,14336]{1,0:T(8,128)(2,1)} fusion(bf16[768,14336]{1,0:T(8,128)(2,1)} %bitcast.73, s32[1024]{0:T(1024)S(1)} %copy-done.15), kind=kCustom, calls=%fused_computation.11.clone | custom fusion | bytes 44043264 | tf_op jit(solution)/shard_map/jit(_take)/gather | solution.py:62
  2492.8 57.5 %gather_fusion.16 = bf16[768,14336]{1,0:T(8,128)(2,1)} fusion(bf16[768,14336]{1,0:T(8,128)(2,1)} %bitcast.74, s32[1024]{0:T(1024)S(1)} %copy-done.15), kind=kCustom, calls=%fused_computation.13.clone | custom fusion | bytes 44043264 | tf_op jit(solution)/shard_map/jit(_take)/gather | solution.py:62
  2550.4 139.3 %all-to-all-done.9 = bf16[32,24,14336]{2,1,0:T(8,128)(2,1)} async-done(((bf16[32,24,14336]{2,1,0:T(8,128)(2,1)}), bf16[32,24,14336]{2,1,0:T(8,128)(2,1)}, u32[]{:S(2)}, u32[]{:S(2)}) %all-to-all-start.9) | async-done | bytes 22020128 | tf_op jit(solution)/shard_map/all_to_all | solution.py:61
  2689.7 57.7 %gather_fusion.18 = bf16[768,14336]{1,0:T(8,128)(2,1)} fusion(bf16[768,14336]{1,0:T(8,128)(2,1)} %bitcast.55, s32[1024]{0:T(1024)S(1)} %copy-done.15), kind=kCustom, calls=%fused_computation.14.clone | custom fusion | bytes 44043264 | tf_op jit(solution)/shard_map/jit(_take)/gather | solution.py:62
  2747.4 42.1 %broadcast_select_fusion = (bf16[768,14336]{1,0:T(8,128)(2,1)}, bf16[768,14336]{1,0:T(8,128)(2,1)}, bf16[768,14336]{1,0:T(8,128)(2,1)}) fusion(bf16[768,14336]{1,0:T(8,128)(2,1)} %gather_fusion.18, pred[768]{0:T(1024)(128)(4,1)S(1)} %copy-done.21, bf16[768,14336]{1,0:T(8,128)(2,1)} %gather_fusion.16, bf16[768,14336]{1,0:T(8,128)(2,1)} %gather_fusion.8), kind=kLoop, calls=%fused_computation.24 | loop fusion | flops 33030144 | bytes 132121344 | tf_op jit(solution)/shard_map/jit(_take)/select_n | solution.py:62
  2960.3 76.8 %all-to-all-done.10 = bf16[32,24,4096]{2,1,0:T(8,128)(2,1)} async-done(((bf16[32,24,4096]{2,1,0:T(8,128)(2,1)}), bf16[32,24,4096]{2,1,0:T(8,128)(2,1)}, u32[]{:S(2)}, u32[]{:S(2)}) %all-to-all-start.10) | async-done | bytes 6291488 | tf_op jit(solution)/shard_map/all_to_all | solution.py:65
  3046.6 48.1 %convolution_add_fusion.4 = f32[256,4096]{1,0:T(8,128)} fusion(bf16[256,14336]{1,0:T(8,128)(2,1)} %get-tuple-element.127, bf16[4096,14336]{1,0:T(8,128)(2,1)} %param.27, bf16[256,4096]{1,0:T(8,128)(2,1)S(1)} %copy-done.2), kind=kOutput, calls=%fused_computation.50 | convolution fusion | flops 30066868224 | bytes 131072000 | tf_op jit(solution)/shard_map/dot_general | solution.py:28
  3207.6 46.8 %fusion.4 = bf16[256,4096]{1,0:T(8,128)(2,1)} fusion(bf16[256,14336]{1,0:T(8,128)(2,1)} %get-tuple-element.128, bf16[14336,4096]{1,0:T(8,128)(2,1)} %param.29, bf16[256,4096]{1,0:T(8,128)(2,1)S(1)} %copy-done.4, bf16[256,4096]{1,0:T(8,128)(2,1)} %gather_fusion.10, pred[256]{0:T(512)(128)(4,1)S(1)} %copy-done.27), kind=kOutput, calls=%fused_computation.54 | convolution fusion | flops 30071062528 | bytes 131072256 | tf_op jit(solution)/shard_map/dot_general | solution.py:81
  3254.3 52.5 %fusion.3 = bf16[256,4096]{1,0:T(8,128)(2,1)} fusion(f32[256,4096]{1,0:T(8,128)} %convolution_add_fusion.4, bf16[256,14336]{1,0:T(8,128)(2,1)} %get-tuple-element.126, bf16[4096,14336]{1,0:T(8,128)(2,1)} %param.28, bf16[256,4096]{1,0:T(8,128)(2,1)} %gather_fusion.20, pred[256]{0:T(512)(128)(4,1)S(1)} %copy-done.27), kind=kOutput, calls=%fused_computation.53 | convolution fusion | flops 30070013952 | bytes 133169408 | tf_op jit(solution)/shard_map/dot_general | solution.py:28
  (185 shorter events, 848.0 us)
Async XLA Ops:
  40.0 39.1 %all-to-all-start.1 = ((s32[32,24,1]{1,2,0:T(1,128)}), s32[32,24,1]{1,2,0:T(1,128)S(1)}, u32[]{:S(2)}, u32[]{:S(2)}) async-start(s32[32,24,1]{1,2,0:T(1,128)} %bitcast.33), calls=%async_computation.1 | async-start | bytes 32768 | tf_op jit(solution)/shard_map/all_to_all | solution.py:55
  163.0 82.8 %all-to-all-start.6 = ((bf16[32,24,4096]{2,1,0:T(8,128)(2,1)}), bf16[32,24,4096]{2,1,0:T(8,128)(2,1)}, u32[]{:S(2)}, u32[]{:S(2)}) async-start(bf16[32,24,4096]{2,1,0:T(8,128)(2,1)} %bitcast.90), calls=%async_computation.6 | async-start | bytes 12582912 | tf_op jit(solution)/shard_map/all_to_all | solution.py:61
  191.2 377.3 %copy-start.12 = (s32[1024]{0:T(1024)}, s32[1024]{0:T(1024)S(1)}, u32[]{:S(2)}) copy-start(s32[1024]{0:T(1024)S(1)} %pad_clamp_fusion.1) | copy-start | bytes 12292
  191.2 70.1 %copy-start.20 = (pred[768]{0:T(1024)(128)(4,1)}, pred[768]{0:T(1024)(128)(4,1)S(1)}, u32[]{:S(2)}) copy-start(pred[768]{0:T(1024)(128)(4,1)S(1)} %compare_and_fusion.1) | copy-start | bytes 2308
  568.5 57.7 %copy-start.18 = (pred[768]{0:T(1024)(128)(4,1)S(1)}, pred[768]{0:T(1024)(128)(4,1)}, u32[]{:S(2)}) copy-start(pred[768]{0:T(1024)(128)(4,1)} %compare_and_fusion) | copy-start | bytes 2308
  668.3 267.6 %slice-start.6 = ((s8[22020096]{0:T(1024)(128)(4,1)}), s8[4194304]{0:T(1024)(128)(4,1)S(1)}, s32[]{:S(2)}) async-start(s8[22020096]{0:T(1024)(128)(4,1)} %bitcast.83), calls=%async_computation.17 | async-start | bytes 8388608
  668.3 267.6 %slice-start.7 = ((s8[22020096]{0:T(1024)(128)(4,1)}), s8[4194304]{0:T(1024)(128)(4,1)S(1)}, s32[]{:S(2)}) async-start(s8[22020096]{0:T(1024)(128)(4,1)} %bitcast.83), calls=%async_computation.18 | async-start | bytes 8388608
  668.3 267.6 %slice-start.8 = ((s8[22020096]{0:T(1024)(128)(4,1)}), s8[4194304]{0:T(1024)(128)(4,1)S(1)}, s32[]{:S(2)}) async-start(s8[22020096]{0:T(1024)(128)(4,1)} %bitcast.83), calls=%async_computation.19 | async-start | bytes 8388608
  668.3 267.6 %slice-start.9 = ((s8[22020096]{0:T(1024)(128)(4,1)}), s8[4194304]{0:T(1024)(128)(4,1)S(1)}, s32[]{:S(2)}) async-start(s8[22020096]{0:T(1024)(128)(4,1)} %bitcast.83), calls=%async_computation.20 | async-start | bytes 8388608
  668.3 267.6 %slice-start.10 = ((s8[22020096]{0:T(1024)(128)(4,1)}), s8[4194304]{0:T(1024)(128)(4,1)S(1)}, s32[]{:S(2)}) async-start(s8[22020096]{0:T(1024)(128)(4,1)} %bitcast.83), calls=%async_computation.21 | async-start | bytes 8388608
  668.4 267.6 %slice-start.11 = ((s8[22020096]{0:T(1024)(128)(4,1)}), s8[1048576]{0:T(1024)(128)(4,1)S(1)}, s32[]{:S(2)}) async-start(s8[22020096]{0:T(1024)(128)(4,1)} %bitcast.83), calls=%async_computation.22 | async-start | bytes 2097152
  1205.6 284.7 %all-to-all-start.7 = ((bf16[32,24,14336]{2,1,0:T(8,128)(2,1)}), bf16[32,24,14336]{2,1,0:T(8,128)(2,1)}, u32[]{:S(2)}, u32[]{:S(2)}) async-start(bf16[32,24,14336]{2,1,0:T(8,128)(2,1)} %bitcast.79), calls=%async_computation.7 | async-start | bytes 44040192 | tf_op jit(solution)/shard_map/all_to_all | solution.py:65
  1219.1 271.1 %copy-start.16 = (s32[1024]{0:T(1024)}, s32[1024]{0:T(1024)S(1)}, u32[]{:S(2)}) copy-start(s32[1024]{0:T(1024)S(1)} %pad_clamp_fusion) | copy-start | bytes 12292
  1610.5 62.9 %copy-start.11 = (s32[1024]{0:T(1024)S(1)}, s32[1024]{0:T(1024)}, u32[]{:S(2)}) copy-start(s32[1024]{0:T(1024)} %copy-done.10) | copy-start | bytes 12292
  1840.9 300.5 %slice-start = ((s8[22020096]{0:T(1024)(128)(4,1)}), s8[4194304]{0:T(1024)(128)(4,1)S(1)}, s32[]{:S(2)}) async-start(s8[22020096]{0:T(1024)(128)(4,1)} %bitcast.80), calls=%async_computation.11 | async-start | bytes 8388608
  1840.9 300.5 %slice-start.1 = ((s8[22020096]{0:T(1024)(128)(4,1)}), s8[4194304]{0:T(1024)(128)(4,1)S(1)}, s32[]{:S(2)}) async-start(s8[22020096]{0:T(1024)(128)(4,1)} %bitcast.80), calls=%async_computation.12 | async-start | bytes 8388608
  1840.9 300.5 %slice-start.2 = ((s8[22020096]{0:T(1024)(128)(4,1)}), s8[4194304]{0:T(1024)(128)(4,1)S(1)}, s32[]{:S(2)}) async-start(s8[22020096]{0:T(1024)(128)(4,1)} %bitcast.80), calls=%async_computation.13 | async-start | bytes 8388608
  1840.9 300.5 %slice-start.3 = ((s8[22020096]{0:T(1024)(128)(4,1)}), s8[4194304]{0:T(1024)(128)(4,1)S(1)}, s32[]{:S(2)}) async-start(s8[22020096]{0:T(1024)(128)(4,1)} %bitcast.80), calls=%async_computation.14 | async-start | bytes 8388608
  1840.9 300.5 %slice-start.4 = ((s8[22020096]{0:T(1024)(128)(4,1)}), s8[4194304]{0:T(1024)(128)(4,1)S(1)}, s32[]{:S(2)}) async-start(s8[22020096]{0:T(1024)(128)(4,1)} %bitcast.80), calls=%async_computation.15 | async-start | bytes 8388608
  1840.9 300.5 %slice-start.5 = ((s8[22020096]{0:T(1024)(128)(4,1)}), s8[1048576]{0:T(1024)(128)(4,1)S(1)}, s32[]{:S(2)}) async-start(s8[22020096]{0:T(1024)(128)(4,1)} %bitcast.80), calls=%async_computation.16 | async-start | bytes 2097152
  2405.0 284.7 %all-to-all-start.9 = ((bf16[32,24,14336]{2,1,0:T(8,128)(2,1)}), bf16[32,24,14336]{2,1,0:T(8,128)(2,1)}, u32[]{:S(2)}, u32[]{:S(2)}) async-start(bf16[32,24,14336]{2,1,0:T(8,128)(2,1)} %bitcast.78), calls=%async_computation.9 | async-start | bytes 44040192 | tf_op jit(solution)/shard_map/all_to_all | solution.py:61
  2933.7 103.4 %all-to-all-start.10 = ((bf16[32,24,4096]{2,1,0:T(8,128)(2,1)}), bf16[32,24,4096]{2,1,0:T(8,128)(2,1)}, u32[]{:S(2)}, u32[]{:S(2)}) async-start(bf16[32,24,4096]{2,1,0:T(8,128)(2,1)} %bitcast.92), calls=%async_computation.10 | async-start | bytes 12582912 | tf_op jit(solution)/shard_map/all_to_all | solution.py:65
  2958.9 87.7 %copy-start.2 = (bf16[256,4096]{1,0:T(8,128)(2,1)S(1)}, bf16[256,4096]{1,0:T(8,128)(2,1)}, u32[]{:S(2)}) copy-start(bf16[256,4096]{1,0:T(8,128)(2,1)} %param.26) | copy-start | bytes 6291460
  3037.1 161.5 %all-to-all-start.5 = ((bf16[32,24,4096]{2,1,0:T(8,128)(2,1)}), bf16[32,24,4096]{2,1,0:T(8,128)(2,1)}, u32[]{:S(2)}, u32[]{:S(2)}) async-start(bf16[32,24,4096]{2,1,0:T(8,128)(2,1)} %bitcast.91), calls=%async_computation.5 | async-start | bytes 12582912 | tf_op jit(solution)/shard_map/all_to_all | solution.py:65
  (22 other events, 441.1 us)
where the time goes:
time: 3320 us; the launch traced here: 3310 us
  blocking collectives  1180 us (36%)
  local copies, waits for them, and re-layouts  678 us (20%)
  waiting for transfers between devices  486 us (15%)
  matrix products  311 us (9%)
  other arithmetic  306 us (9%)
  Pallas kernels  265 us (8%)
  starting transfers between devices  75.5 us (2%)
    all_to_all x3, blocking collectives, to_owner(): arrived = lax.all_to_all(pack_rows(in_rows), 'data', 0, 0, tiled=True)  648 us
    all_to_all x2, blocking collectives, to_source(): lax.all_to_all(jnp.take(owner_rows, restore, axis=0), 'data', 0, 0, tiled...  537 us
    all_to_all x3, waiting for transfers between devices, to_source(): lax.all_to_all(jnp.take(owner_rows, restore, axis=0), 'data', 0, 0, tiled...  308 us
    gather x5, local copies, waits for them, and re-layouts, to_source(): jnp.take(owner_rows, restore, axis=0)  204 us
    gather x5, local copies, waits for them, and re-layouts, to_owner(): return jnp.take(arrived, sort_order, axis=0)  204 us
    all_to_all x2, waiting for transfers between devices, to_owner(): arrived = lax.all_to_all(pack_rows(in_rows), 'data', 0, 0, tiled=True)  178 us
    another operation x12, Pallas kernels  175 us
    dot_general x3, matrix products, contract_last(): lax.dot_general(left_rows, weight, (((1,), (1,)), ((), ())), preferred_el...  164 us
  transfers between devices with their start and end apart: 6, of which 4 were waited for; matrix products, arithmetic and copies ran while one was open for 9% of the time, Pallas kernels for 2%

commit v1 on v0

v1 whole, which is shorter than its diff:
```python
import functools

import jax
import jax.numpy as jnp
from jax import lax
from jax.experimental import pallas as pl
from jax.experimental.pallas import tpu as pltpu
from jax.sharding import PartitionSpec as P

ALPHA = 32
LANES = 128
F32 = jnp.float32
BF16 = jnp.bfloat16
VMEM_LIMIT = 62 * 1024 * 1024


def dot_nn(a, b):
    return lax.dot_general(a, b, (((1,), (0,)), ((), ())), preferred_element_type=F32)


def dot_nt(a, b):
    return lax.dot_general(a, b, (((1,), (1,)), ((), ())), preferred_element_type=F32)


def dot_tn(a, b):
    return lax.dot_general(a, b, (((0,), (0,)), ((), ())), preferred_element_type=F32)


def whole(shape):
    return pl.BlockSpec(shape, lambda *_: (0,) * len(shape), pipeline_mode=pl.Buffered(1))


def params(**kw):
    return pltpu.CompilerParams(vmem_limit_bytes=VMEM_LIMIT, **kw)


def cost(flops, nbytes):
    return pl.CostEstimate(flops=flops, bytes_accessed=nbytes, transcendentals=0)


MESH_ID = pl.DeviceIdType.MESH


class Exchange:
    def __init__(self, groups, items, collective_id):
        self.groups, self.items, self.collective_id = groups, items, collective_id
        self.arrays = [a for _, a, _ in items]
        self.rows = [a.shape[0] // {'block': groups, 'some': max(n, 1), 'all': 1}[kind] for kind, a, n in items]
        self.out_shape = [jax.ShapeDtypeStruct((groups * b, a.shape[1]), a.dtype) for b, a in zip(self.rows, self.arrays, strict=True)]
        self.specs = [pl.BlockSpec(memory_space=pl.ANY)] * len(items)
        self.scratch = [pltpu.SemaphoreType.DMA((len(items),))] * 2

    def params(self):
        return params(collective_id=self.collective_id, has_side_effects=True)

    def start(self, srcs, dsts, send, recv):
        groups = self.groups
        me = lax.axis_index('data')
        barrier = pltpu.get_barrier_semaphore()

        def signal(i, _):
            pl.semaphore_signal(barrier, inc=1, device_id={'data': lax.rem(me + i, groups)}, device_id_type=MESH_ID)
            return 0

        lax.fori_loop(1, groups, signal, 0)
        pl.semaphore_wait(barrier, groups - 1)
        for k, (kind, _, n) in enumerate(self.items):
            b = self.rows[k]

            def part(dest, k=k, b=b, kind=kind):
                return srcs[k] if kind == 'all' else srcs[k].at[pl.ds(dest * b, b)]

            def copy(dest, k=k, b=b, part=part):
                pltpu.make_async_remote_copy(
                    src_ref=part(dest), dst_ref=dsts[k].at[pl.ds(me * b, b)], send_sem=send.at[k], recv_sem=recv.at[k],
                    device_id={'data': dest}, device_id_type=MESH_ID).start()

            def mine(k=k, b=b, part=part):
                pltpu.make_async_copy(part(me), dsts[k].at[pl.ds(me * b, b)], recv.at[k]).start()

            def step(i, _, copy=copy, kind=kind, n=n):
                dest = lax.rem(me + i, groups)
                if kind == 'some' and n < groups:
                    pl.when(dest < n)(lambda: copy(dest))
                else:
                    copy(dest)
                return 0

            lax.fori_loop(1, groups, step, 0)
            if kind == 'some' and n < groups:
                pl.when(me < n)(mine)
            else:
                mine()

    def finish(self, srcs, dsts, send, recv):
        groups = self.groups
        me = lax.axis_index('data')
        for k, (kind, _, n) in enumerate(self.items):
            b = self.rows[k]

            def took(count, sem, k=k, b=b):
                ref = dsts[k].at[pl.ds(0, count * b)]
                pltpu.make_async_copy(ref, ref, sem.at[k]).wait()

            if kind == 'some' and n < groups:
                pl.when(me < n)(lambda took=took: took(groups, recv))
                pl.when(me < n)(lambda took=took, n=n: took(n - 1, send))
                pl.when(me >= n)(lambda took=took, n=n: took(n, send))
            else:
                took(groups, recv)
                took(groups - 1, send)


def exchange_kernel(*refs, xchg):
    n = len(xchg.items)
    srcs, dsts, sems = refs[:n], refs[n:2 * n], refs[2 * n:]
    xchg.start(srcs, dsts, *sems)
    xchg.finish(srcs, dsts, *sems)


def exchange_only(xchg):
    return pl.pallas_call(
        functools.partial(exchange_kernel, xchg=xchg),
        in_specs=xchg.specs,
        out_specs=xchg.specs,
        out_shape=xchg.out_shape,
        scratch_shapes=xchg.scratch,
        compiler_params=xchg.params(),
        cost_estimate=cost(10**10, 10**7),
        name='exchange',
    )(*xchg.arrays)


def route_kernel(own_ref, ids_ref, x_ref, d_ref, xp_ref, dp_ref, meta_ref, pt_ref, *, groups):
    tokens = ids_ref.shape[1]
    quota = tokens // groups
    sq = (tokens, tokens)
    row = lax.broadcasted_iota(jnp.int32, sq, 0)
    col = lax.broadcasted_iota(jnp.int32, sq, 1)
    slot_owner_r = lax.div(row, jnp.int32(quota))
    slot_owner_c = lax.div(col, jnp.int32(quota))
    own_c = jnp.broadcast_to(own_ref[...], sq)
    own_r = own_c.T
    one = jnp.float32(1)
    zero = jnp.float32(0)

    def count(cond, axis):
        return jnp.sum(jnp.where(cond, one, zero), axis=axis, keepdims=True)

    rank_c = count((own_c == own_r) & (row < col), 0)
    rank_r = count((own_c == own_r) & (col < row), 1)
    over_c = rank_c >= quota
    over_r = jnp.broadcast_to(rank_r, sq) >= quota
    over_idx_c = count(over_r & (row < col), 0)
    held_r = count(own_c == slot_owner_r, 1)
    held_c = count(own_r == slot_owner_c, 0)
    place_r = (row - slot_owner_r * quota).astype(F32)
    place_c = (col - slot_owner_c * quota).astype(F32)
    free_r = place_r >= held_r
    free_c = place_c >= held_c
    free_idx_r = count(free_c & (col < row), 1)
    own_cf = own_c.astype(F32)
    near = (own_cf * quota + rank_c) == row.astype(F32)
    spare = free_r & (free_idx_r == over_idx_c)
    over_cf = jnp.broadcast_to(jnp.where(over_c, one, zero), sq)
    perm = jnp.where(over_cf > 0, jnp.where(spare, one, zero), jnp.where(near, one, zero))
    perm_b = perm.astype(BF16)
    xp_ref[...] = dot_nn(perm_b, x_ref[...]).astype(BF16)
    dp_ref[...] = dot_nn(perm_b, d_ref[...]).astype(BF16)
    pt_ref[...] = perm.T.astype(BF16)
    ids_r = jnp.sum(perm * ids_ref[...].astype(F32), axis=1, keepdims=True)
    hot_max = jnp.max(jnp.where(over_cf > 0, own_cf, -one))
    hot_min = jnp.min(jnp.where(over_cf > 0, own_cf, one * groups))
    lane = lax.broadcasted_iota(jnp.int32, meta_ref.shape, 1)
    meta_ref[...] = jnp.where(lane == 0, ids_r, jnp.where(lane == 1, hot_max, hot_min))


def route(ids, owner, x, dy, groups):
    tokens, width = x.shape
    return pl.pallas_call(
        functools.partial(route_kernel, groups=groups),
        out_shape=(
            jax.ShapeDtypeStruct(x.shape, BF16),
            jax.ShapeDtypeStruct(dy.shape, BF16),
            jax.ShapeDtypeStruct((tokens, LANES), F32),
            jax.ShapeDtypeStruct((tokens, tokens), BF16),
        ),
        compiler_params=params(),
        cost_estimate=cost(4 * tokens * tokens * width, 8 * tokens * width),
        name='route',
    )(owner.reshape(1, tokens), ids.reshape(1, tokens), x, dy)


def back_kernel(pt_ref, out_in, dxa_in, dxb_in, out_ref, dx_ref):
    pt = pt_ref[...]
    half = dxa_in.shape[1]
    out_ref[...] = dot_nn(pt, out_in[...]).astype(BF16)
    dx_ref[:, :half] = dot_nn(pt, dxa_in[...]).astype(BF16)
    dx_ref[:, half:] = dot_nn(pt, dxb_in[...]).astype(BF16)


def back(pt, out, dxa, dxb):
    tokens, width = out.shape
    return pl.pallas_call(
        back_kernel,
        out_shape=[jax.ShapeDtypeStruct(out.shape, BF16)] * 2,
        compiler_params=params(),
        cost_estimate=cost(4 * tokens * tokens * width, 8 * tokens * width),
        name='back',
    )(pt, out, dxa, dxb)


def gu_kernel(x_ref, wg_ref, wu_ref, *refs, xchg, steps, old):
    n = len(xchg.items)
    srcs, refs = refs[:n], refs[n + old:]
    (g_ref, u_ref), dsts, sems = refs[:2], refs[2:n + 2], refs[n + 2:]
    step = pl.program_id(0)

    @pl.when(step == 0)
    def _():
        xchg.start(srcs, dsts, *sems)

    x = x_ref[...]
    g_ref[...] = dot_nn(x, wg_ref[...])
    u_ref[...] = dot_nn(x, wu_ref[...])

    @pl.when(step == steps - 1)
    def _():
        xchg.finish(srcs, dsts, *sems)


def gate_up(x, wg, wu, tile, start, steps, total, xchg, old=()):
    tokens, width = x.shape
    cols = tile * steps
    at = lambda i: (0, start + i)
    n = len(xchg.items)
    return pl.pallas_call(
        functools.partial(gu_kernel, xchg=xchg, steps=steps, old=len(old)),
        grid=(steps,),
        in_specs=[whole(x.shape)] + [pl.BlockSpec((width, tile), at)] * 2 + xchg.specs + [pl.BlockSpec(memory_space=pl.ANY)] * len(old),
        out_specs=[pl.BlockSpec((tokens, tile), at)] * 2 + xchg.specs,
        out_shape=[jax.ShapeDtypeStruct((tokens, tile * total), F32)] * 2 + xchg.out_shape,
        scratch_shapes=xchg.scratch,
        input_output_aliases={3 + n + k: k for k in range(len(old))},
        compiler_params=xchg.params(),
        cost_estimate=cost(4 * tokens * width * cols, 4 * width * cols + 8 * tokens * cols),
        name='gate_up',
    )(x, wg, wu, *xchg.arrays, *old)


def adapter_mask(scal_ref, meta_ref, rank, n_local, cols):
    me, hot = scal_ref[0], scal_ref[1]
    shape = (meta_ref.shape[0], cols)
    lid = jnp.broadcast_to(meta_ref[:, 0:1], shape).astype(jnp.int32)
    col = lax.broadcasted_iota(jnp.int32, shape, 1)
    block = lax.div(col, jnp.int32(rank))
    mine = me * n_local + block
    theirs = jnp.where(hot == me, -1, hot * n_local + block - n_local)
    return jnp.where(block < n_local, mine, theirs) == lid


def mid_kernel(*refs, names, cfg, xchg):
    r = dict(zip(names, refs, strict=True))
    first, last, steps = cfg['first'], cfg['last'], cfg['steps']
    rank, n_local, scale, groups = cfg['rank'], cfg['n_local'], cfg['scale'], cfg['groups']
    half = rank * n_local
    cap = cfg['cap']
    step = pl.program_id(0)
    count = len(xchg.items) if xchg else 0
    srcs = [r['x_src%d' % k] for k in range(count)]
    dsts = [r['x_dst%d' % k] for k in range(count)]

    def scaled(v):
        return v if scale == 1.0 else v * scale

    def both(name):
        return jnp.concatenate([r[name + '_own'][...], r[name + '_hot'][...]], axis=0)

    def packed(values, tail):
        parts = []
        for v in values:
            rows = dot_nn(r['sel'][...], v[:, half:])
            parts.append(sum(rows[:, k * rank:(k + 1) * rank] for k in range(n_local)))
        return jnp.concatenate([*parts, tail], axis=1).astype(BF16)

    @pl.when(step == 0)
    def _():
        if xchg:
            xchg.start(srcs, dsts, r['send'], r['recv'])
        if first:
            me, hot = r['scal'][0], r['scal'][1]
            mask = adapter_mask(r['scal'], r['meta'], rank, n_local, 2 * half)
            r['pg'][...] = jnp.where(mask, dot_nt(r['x'][...], both('ag')), 0.0).astype(BF16)
            r['pu'][...] = jnp.where(mask, dot_nt(r['x'][...], both('au')), 0.0).astype(BF16)
            r['qd'][...] = jnp.where(mask, scaled(dot_nt(r['dy'][...], both('bd'))), 0.0).astype(BF16)
            for name in ('pd_acc', 'qg_acc', 'qu_acc', 'out_acc'):
                r[name][...] = jnp.zeros_like(r[name])
            tokens = r['meta'].shape[0]
            sq = (tokens, tokens)
            low = (me * n_local).astype(F32)
            far = lambda lid: jnp.where((lid < low) | (lid >= low + n_local), 1.0, 0.0)
            lid_r = jnp.broadcast_to(r['meta'][:, 0:1], sq)
            before = lax.broadcasted_iota(jnp.int32, sq, 0) < lax.broadcasted_iota(jnp.int32, sq, 1)
            nth = jnp.sum(jnp.where(before, far(lid_r), 0.0), axis=0, keepdims=True)
            lid_c = lid_r.T[0:1]
            far_c = far(lid_c)
            slot = lax.broadcasted_iota(jnp.int32, (cap, tokens), 0).astype(F32)
            sel = jnp.where(slot == nth, jnp.broadcast_to(far_c, (cap, tokens)), 0.0)
            r['sel'][...] = sel.astype(BF16)
            which = jnp.sum(sel * (lid_c - (hot * n_local).astype(F32)), axis=1, keepdims=True)
            lane = lax.broadcasted_iota(jnp.int32, (cap, rank), 1)
            tail = jnp.where(lane == 0, which, jnp.where(lane == 1, jnp.sum(far_c), 0.0))
            r['prow'][...] = packed([r['pg'][...], r['pu'][...], r['qd'][...]], tail)
            for k, name in enumerate(('pg', 'pu', 'qd')):
                r['left'][k] = jnp.concatenate([r[name][:, :half].astype(F32).T, sel], axis=0).astype(BF16)
            part = r['x'].shape[1] // groups
            for k, name in enumerate(('x', 'dy')):
                rows = dot_nn(r['sel'][...], r[name][...]).astype(BF16)
                for d in range(groups):
                    r['drow'][d * cap:(d + 1) * cap, k * part:(k + 1) * part] = rows[:, d * part:(d + 1) * part]
        else:
            for name in ('pg', 'pu', 'qd', 'sel', 'left', 'pd_acc', 'qg_acc', 'qu_acc', 'out_acc'):
                r[name][...] = r[name + '_in'][...]

    pg, pu, qd = r['pg'][...], r['pu'][...], r['qd'][...]
    bg, bu, ad, wd = both('bg'), both('bu'), both('ad'), r['wd'][...]
    g = r['g'][...] + scaled(dot_nn(pg, bg)).astype(BF16).astype(F32)
    u = r['u'][...] + scaled(dot_nn(pu, bu)).astype(BF16).astype(F32)
    dh = dot_nt(r['dy'][...], wd) + dot_nn(qd, ad).astype(BF16).astype(F32)
    sig = jax.nn.sigmoid(g)
    act = g * sig
    h = (act * u).astype(BF16)
    dg = (dh * u * sig * (1.0 + g * (1.0 - sig))).astype(BF16)
    du = (dh * act).astype(BF16)
    r['dg'][...] = dg
    r['du'][...] = du
    r['pd_acc'][...] += dot_nt(h, ad)
    r['qg_acc'][...] += dot_nt(dg, bg)
    r['qu_acc'][...] += dot_nt(du, bu)
    r['out_acc'][...] += dot_nn(h, wd)
    piece = h.shape[1] // 2
    for k, (name, left, v) in enumerate((('gad', 2, h), ('gbg', 0, dg), ('gbu', 1, du))):
        both_rows = dot_nn(r['left'][left], v)
        r[name][...] = both_rows[:half] if name == 'gad' else scaled(both_rows[:half])
        for i in range(2):
            r['rows'][i * cap:(i + 1) * cap, k * piece:(k + 1) * piece] = both_rows[half:, i * piece:(i + 1) * piece].astype(BF16)

    @pl.when(step == steps - 1)
    def _():
        if last:
            mask = adapter_mask(r['scal'], r['meta'], rank, n_local, 2 * half)
            pd = jnp.where(mask, r['pd_acc'][...], 0.0).astype(BF16)
            qg = jnp.where(mask, scaled(r['qg_acc'][...]), 0.0).astype(BF16)
            qu = jnp.where(mask, scaled(r['qu_acc'][...]), 0.0).astype(BF16)
            r['qg'][...] = qg
            r['qu'][...] = qu
            e_down = scaled(dot_nn(pd, both('bd'))).astype(BF16).astype(F32)
            r['out'][...] = (r['x'][...].astype(F32) + r['out_acc'][...] + e_down).astype(BF16)
            r['gag'][...] = dot_tn(qg[:, :half], r['x'][...])
            r['gau'][...] = dot_tn(qu[:, :half], r['x'][...])
            r['gbd'][...] = scaled(dot_tn(pd[:, :half], r['dy'][...]))
            r['prow'][...] = packed([qg, qu, pd], jnp.zeros((cap, rank), F32))
        if xchg:
            xchg.finish(srcs, dsts, r['send'], r['recv'])


def mid(arrays, cfg, xchg=None):
    first, last = cfg['first'], cfg['last']
    tile, start, steps, cap, groups = cfg['tile'], cfg['start'], cfg['steps'], cfg['cap'], cfg['groups']
    tokens, width = arrays['x'].shape
    hidden = arrays['wd'].shape[0]
    rank = cfg['rank']
    half = rank * cfg['n_local']
    cols = tile * steps
    at = lambda i: (0, start + i)
    anywhere = pl.BlockSpec(memory_space=pl.ANY)
    ins, specs, aliases = [], [], {}

    def take(name, spec):
        ins.append(name)
        specs.append(spec)

    take('scal', pl.BlockSpec(memory_space=pltpu.SMEM))
    for name in ('meta', 'x', 'dy'):
        take(name, whole(arrays[name].shape))
    for name in ('ag', 'au', 'bd') if first else ('bd',):
        take(name + '_own', whole((half, width)))
        take(name + '_hot', whole((half, width)))
    carry = [('pg', BF16, (tokens, 2 * half)), ('pu', BF16, (tokens, 2 * half)), ('qd', BF16, (tokens, 2 * half)),
             ('sel', BF16, (cap, tokens)), ('left', BF16, (3, half + cap, tokens)),
             ('pd_acc', F32, (tokens, 2 * half)), ('qg_acc', F32, (tokens, 2 * half)), ('qu_acc', F32, (tokens, 2 * half)),
             ('out_acc', F32, (tokens, width))]
    if not first:
        for name, _, shape in carry:
            take(name + '_in', whole(shape))
    for name in ('bg', 'bu', 'ad'):
        take(name + '_own', pl.BlockSpec((half, tile), at))
        take(name + '_hot', pl.BlockSpec((half, tile), at))
    take('wd', pl.BlockSpec((tile, width), lambda i: (start + i, 0)))
    for name in ('g', 'u'):
        take(name, pl.BlockSpec((tokens, tile), at))
    outs, ospecs, oshapes = [], [], []

    def give(name, shape, dtype, spec):
        outs.append(name)
        ospecs.append(spec)
        oshapes.append(jax.ShapeDtypeStruct(shape, dtype))

    wide = [(name, (half, hidden), F32, half) for name in ('gbg', 'gbu', 'gad')] + [(name, (tokens, hidden), BF16, tokens) for name in ('dg', 'du')]
    for name, shape, dtype, n in wide:
        give(name, shape, dtype, pl.BlockSpec((n, tile), at))
        if not first:
            aliases[len(ins)] = outs.index(name)
            take(name + '_in', anywhere)
    give('rows', (2 * steps * cap, 3 * tile // 2), BF16, pl.BlockSpec((2 * cap, 3 * tile // 2), lambda i: (i, 0)))
    give('prow', (cap, 4 * rank), BF16, whole((cap, 4 * rank)))
    scratch = []
    if first:
        give('drow', (groups * cap, 2 * width // groups), BF16, whole((groups * cap, 2 * width // groups)))
    if last:
        give('out', (tokens, width), BF16, whole((tokens, width)))
        for name in ('qg', 'qu'):
            give(name, (tokens, 2 * half), BF16, whole((tokens, 2 * half)))
        for name in ('gag', 'gau', 'gbd'):
            give(name, (half, width), F32, whole((half, width)))
        scratch = [(name, pltpu.VMEM(shape, dtype)) for name, dtype, shape in carry]
    else:
        for name, dtype, shape in carry:
            give(name, shape, dtype, whole(shape))
    if xchg:
        for k, (array, shape) in enumerate(zip(xchg.arrays, xchg.out_shape, strict=True)):
            arrays = {**arrays, 'x_src%d' % k: array}
            take('x_src%d' % k, anywhere)
            give('x_dst%d' % k, shape.shape, shape.dtype, anywhere)
        scratch += list(zip(('send', 'recv'), xchg.scratch, strict=True))
    names = ins + outs + [name for name, _ in scratch]
    results = pl.pallas_call(
        functools.partial(mid_kernel, names=names, cfg=cfg, xchg=xchg),
        grid=(steps,),
        in_specs=specs,
        out_specs=ospecs,
        out_shape=oshapes,
        scratch_shapes=[s for _, s in scratch],
        input_output_aliases=aliases,
        compiler_params=xchg.params() if xchg else params(),
        cost_estimate=cost(4 * tokens * width * cols, 2 * width * cols),
        name='mid',
    )(*[arrays[name] for name in ins])
    return dict(zip(outs, results, strict=True))


def dx_kernel(dy_ref, qg_ref, qu_ref, ag_own, ag_hot, au_own, au_hot, dg_ref, du_ref, wg_ref, wu_ref, *refs, xchg, steps):
    n = len(xchg.items)
    srcs, dx_ref, dsts, send, recv = refs[:n], refs[n], refs[n + 1:2 * n + 1], refs[-2], refs[-1]
    step = pl.program_id(0)

    @pl.when(step == 0)
    def _():
        xchg.start(srcs, dsts, send, recv)

    ag = jnp.concatenate([ag_own[...], ag_hot[...]], axis=0)
    au = jnp.concatenate([au_own[...], au_hot[...]], axis=0)
    low = (dot_nn(qg_ref[...], ag) + dot_nn(qu_ref[...], au)).astype(BF16).astype(F32)
    base = dot_nt(dg_ref[...], wg_ref[...]) + dot_nt(du_ref[...], wu_ref[...])
    dx_ref[...] = (dy_ref[...].astype(F32) + base + low).astype(BF16)

    @pl.when(step == steps - 1)
    def _():
        xchg.finish(srcs, dsts, send, recv)


def dx_part(dy, qg, qu, ag_own, ag_hot, au_own, au_hot, dg, du, wg, wu, tile, start, steps, xchg):
    tokens = dy.shape[0]
    hidden = dg.shape[1]
    half = ag_own.shape[0]
    width = steps * tile
    at = lambda i: (0, start + i)
    return pl.pallas_call(
        functools.partial(dx_kernel, xchg=xchg, steps=steps),
        grid=(steps,),
        in_specs=[pl.BlockSpec((tokens, tile), at), whole(qg.shape), whole(qu.shape)]
        + [pl.BlockSpec((half, tile), at)] * 4
        + [whole(dg.shape), whole(du.shape)]
        + [pl.BlockSpec((tile, hidden), lambda i: (start + i, 0))] * 2
        + xchg.specs,
        out_specs=[pl.BlockSpec((tokens, tile), lambda i: (0, i))] + xchg.specs,
        out_shape=[jax.ShapeDtypeStruct((tokens, width), BF16)] + xchg.out_shape,
        scratch_shapes=xchg.scratch,
        compiler_params=xchg.params(),
        cost_estimate=cost(4 * tokens * width * hidden, 4 * width * hidden),
        name='dx',
    )(dy, qg, qu, ag_own, ag_hot, au_own, au_hot, dg, du, wg, wu, *xchg.arrays)


def slice_kernel(scal_ref, rows_ref, early_ref, *refs, rank, n_local, count, scale, deep):
    out_ref = refs[-1]
    half = rank * n_local
    piece = rows_ref.shape[1] // 3
    live = scal_ref[0] < count
    which = early_ref[:, 3 * rank:3 * rank + 1].astype(F32)

    def p(ref, k):
        v = ref[:, k * rank:(k + 1) * rank].astype(F32)
        return jnp.concatenate([jnp.where(which == i, v, 0.0) for i in range(n_local)], axis=1).astype(BF16)

    row = lambda k: rows_ref[:, k * piece:(k + 1) * piece]
    wide = (scale * dot_tn(p(early_ref, 0), row(1)), scale * dot_tn(p(early_ref, 1), row(2)), dot_tn(p(early_ref, 2), row(0)))
    for k, v in enumerate(wide):
        out_ref[k * half:(k + 1) * half, :piece] = jnp.where(live, v, 0.0)
    if deep:
        late_ref, drow_ref = refs[:2]
        x, dy = drow_ref[:, :deep], drow_ref[:, deep:]
        for k, v in enumerate((dot_tn(p(late_ref, 0), x), dot_tn(p(late_ref, 1), x), scale * dot_tn(p(late_ref, 2), dy))):
            out_ref[k * half:(k + 1) * half, piece:] = v


def slices(scal, rows, early, more, rank, n_local, count, scale):
    piece = rows.shape[1] // 3
    deep = more[1].shape[1] // 2 if more else 0
    return pl.pallas_call(
        functools.partial(slice_kernel, rank=rank, n_local=n_local, count=count, scale=scale, deep=deep),
        in_specs=[pl.BlockSpec(memory_space=pltpu.SMEM)] + [pl.BlockSpec(memory_space=pltpu.VMEM)] * (2 + len(more)),
        out_shape=jax.ShapeDtypeStruct((3 * rank * n_local, piece + deep), F32),
        compiler_params=params(),
        cost_estimate=cost(10**9, 10**7),
        name='slices',
    )(scal, rows, early, *more)


def add_kernel(flag_ref, *refs, half, heads):
    own, (more_a, more_b, more_d), outs = refs[:6], refs[6:9], refs[9:]
    step = pl.program_id(0)

    def put(k, out, mine, source):
        n, _, piece = source.shape
        for p in range(n):
            cols = slice(p * piece, (p + 1) * piece)
            out[:, cols] = mine[:, cols] + source[p, k * half:(k + 1) * half]

    for k in range(3):
        for mine, out, source, when in (
            (own[k], outs[k], more_a, step < heads), (own[k], outs[k], more_b, step >= heads), (own[3 + k], outs[3 + k], more_d, None)):
            hot = flag_ref[0] > 0
            pl.when(hot if when is None else hot & when)(functools.partial(put, k, out, mine, source))

        @pl.when(flag_ref[0] <= 0)
        def _(k=k):
            outs[k][...] = own[k][...]
            outs[3 + k][...] = own[3 + k][...]


def add_if(flag, own, more_a, more_b, half, piece, deep, n_a, n_b, groups):
    many, many_d = 1024 // piece, max(1, min(groups, 1024 // deep))
    tile, tile_d = many * piece, many_d * deep
    steps_a, steps_b, steps_d = n_a // many, n_b // many, groups // many_d
    wide = pl.BlockSpec((half, tile), lambda i, f: (0, i))
    narrow = pl.BlockSpec((half, tile_d), lambda i, f: (0, jnp.minimum(i, steps_d - 1)))
    cube = lambda a: a.reshape(groups, 3 * half, a.shape[1])
    rows = 3 * half
    specs = [wide] * 3 + [narrow] * 3
    return pl.pallas_call(
        functools.partial(add_kernel, half=half, heads=steps_a),
        grid_spec=pltpu.PrefetchScalarGridSpec(
            num_scalar_prefetch=1, grid=(steps_a + steps_b,),
            in_specs=specs + [
                pl.BlockSpec((many, rows, piece), lambda i, f: (jnp.minimum(i, steps_a - 1) * f[0], 0, 0)),
                pl.BlockSpec((many, rows, piece), lambda i, f: (jnp.maximum(i - steps_a, 0) * f[0], 0, 0)),
                pl.BlockSpec((many_d, rows, deep), lambda i, f: (jnp.minimum(i, steps_d - 1) * f[0], 0, piece // deep)),
            ],
            out_specs=specs),
        out_shape=[jax.ShapeDtypeStruct(a.shape, F32) for a in own],
        compiler_params=params(),
        name='add_if',
    )(flag, *own, cube(more_a), cube(more_b), cube(more_b))


def small_dot_kernel(a_ref, b_ref, o_ref, *, dot):
    @pl.when(pl.program_id(1) == 0)
    def _():
        o_ref[...] = jnp.zeros_like(o_ref)

    o_ref[...] += dot(a_ref[...], b_ref[...])


def small_dot(a, b, dot):
    a_at, b_at = (0 if dot is dot_tn else 1), (1 if dot is dot_nt else 0)
    depth, rows, cols = a.shape[a_at], a.shape[1 - a_at], b.shape[1 - b_at]
    bk, bn = min(depth, 512), min(cols, 512)
    a_spec = pl.BlockSpec((bk, rows), lambda j, k: (k, 0)) if a_at == 0 else pl.BlockSpec((rows, bk), lambda j, k: (0, k))
    b_spec = pl.BlockSpec((bk, bn), lambda j, k: (k, j)) if b_at == 0 else pl.BlockSpec((bn, bk), lambda j, k: (j, k))
    return pl.pallas_call(
        functools.partial(small_dot_kernel, dot=dot),
        grid=(cols // bn, depth // bk),
        in_specs=[a_spec, b_spec],
        out_specs=pl.BlockSpec((rows, bn), lambda j, k: (0, j)),
        out_shape=jax.ShapeDtypeStruct((rows, cols), F32),
        compiler_params=params(),
        name='small_dot',
    )(a, b)


def ring_path(x, ids, dy, wg, wu, wd, ag, bg, au, bu, ad, bd, groups, n_local, scale):
    rank = ag.shape[0] // n_local
    dot_nn_, dot_nt_, dot_tn_ = (functools.partial(small_dot, dot=d) for d in (dot_nn, dot_nt, dot_tn))
    half = rank * n_local
    me = lax.axis_index('data')
    ring = [(i, (i + 1) % groups) for i in range(groups)]
    shift = functools.partial(lax.ppermute, axis_name='data', perm=ring)
    tokens, width = x.shape
    hidden = wd.shape[0]

    def mask_of(k):
        owner = lax.rem(me - k + groups, groups)
        return ids[:, None] == owner * n_local + (jnp.arange(half) // rank)[None, :]

    def low(v, mask):
        return jnp.where(mask, v, 0.0).astype(BF16)

    def forward(k, carry):
        (cag, cbg, cau, cbu, cad, cbd), eg, eu, dh = carry
        mask = mask_of(k)
        eg = eg + scale * dot_nn_(low(dot_nt_(x, cag), mask), cbg)
        eu = eu + scale * dot_nn_(low(dot_nt_(x, cau), mask), cbu)
        dh = dh + dot_nn_(low(scale * dot_nt_(dy, cbd), mask), cad)
        return jax.tree.map(shift, (cag, cbg, cau, cbu, cad, cbd)), eg, eu, dh

    zero = jnp.zeros((tokens, hidden), F32)
    held, eg, eu, dh_low = lax.fori_loop(0, groups, forward, ((ag, bg, au, bu, ad, bd), zero, zero, zero))
    rounded = lambda v: v.astype(BF16).astype(F32)
    g = dot_nn_(x, wg) + rounded(eg)
    u = dot_nn_(x, wu) + rounded(eu)
    sig = jax.nn.sigmoid(g)
    act = g * sig
    h = (act * u).astype(BF16)
    dh = dot_nt_(dy, wd) + rounded(dh_low)
    dg = (dh * u * sig * (1.0 + g * (1.0 - sig))).astype(BF16)
    du = (dh * act).astype(BF16)

    def backward(k, carry):
        held, sums, e_down, dx_low = jax.tree.map(shift, carry[:2]) + carry[2:]
        cag, cbg, cau, cbu, cad, cbd = held
        mask = mask_of(k)
        pg, pu, pd = (low(dot_nt_(a, b), mask) for a, b in ((x, cag), (x, cau), (h, cad)))
        qg, qu, qd = (low(scale * dot_nt_(a, b), mask) for a, b in ((dg, cbg), (du, cbu), (dy, cbd)))
        e_down = e_down + scale * dot_nn_(pd, cbd)
        dx_low = dx_low + dot_nn_(qg, cag) + dot_nn_(qu, cau)
        more = (dot_tn_(qg, x), scale * dot_tn_(pg, dg), dot_tn_(qu, x), scale * dot_tn_(pu, du), dot_tn_(qd, h), scale * dot_tn_(pd, dy))
        return held, tuple(s + m for s, m in zip(sums, more, strict=True)), e_down, dx_low

    sums = tuple(jnp.zeros(a.shape, F32) for a in (ag, bg, au, bu, ad, bd))
    zero = jnp.zeros((tokens, width), F32)
    _, sums, e_down, dx_low = lax.fori_loop(1, groups + 1, backward, (held, sums, zero, zero))
    out = (x.astype(F32) + dot_nn_(h, wd) + rounded(e_down)).astype(BF16)
    dx = (dy.astype(F32) + dot_nt_(dg, wg) + dot_nt_(du, wu) + rounded(dx_low)).astype(BF16)
    return (out, dx, *sums)


def solution(mesh, force_ring=False, split=4 / 7):
    groups = mesh.shape['data']
    tok_spec = P(('rep', 'data'), None)
    own_spec = P('data', None, None)
    grad_spec = P(('rep', 'data'), None, None)

    def device_fn(x, ids, dy, wg, wu, wd, a_gate, b_gate, a_up, b_up, a_down, b_down):
        tokens, width = x.shape
        hidden = wg.shape[1]
        n_local, _, rank = a_gate.shape
        half = n_local * rank
        scale = ALPHA / rank
        me = lax.axis_index('data')
        tall = lambda a: jnp.transpose(a, (0, 2, 1)).reshape(half, a.shape[1])
        flat = lambda a: a.reshape(half, a.shape[2])
        own = dict(ag=tall(a_gate), bg=flat(b_gate), au=tall(a_up), bu=flat(b_up), ad=tall(a_down), bd=flat(b_down))

        xp, dp, meta, pt = route(ids, lax.div(ids, n_local), x, dy, groups)
        me_f = me.astype(F32)
        i_am_hot = (meta[0, 1] == me_f) & (meta[0, 2] == me_f)
        tile = 512
        tiles = hidden // tile
        head = max(2, min(tiles - 2, groups // 2, 2 * round(tiles * split / 2)))
        hot = lax.psum({k: jnp.where(i_am_hot, v, jnp.zeros_like(v)) for k, v in own.items()}, 'data')
        xr, meta_r = exchange_only(Exchange(groups, [('block', xp, 0), ('block', meta, 0)], 0))

        hot_all, low_all = meta_r[:, 1], meta_r[:, 2]
        hot_f = jnp.max(hot_all)
        hot_id = hot_f.astype(jnp.int32)
        scal = jnp.stack([me, hot_id]).astype(jnp.int32)
        flag = jnp.where(hot_id == me, 1, 0).astype(jnp.int32).reshape(1)

        cap = 24
        wider = 2 * tile if tiles % 2 == 0 else tile
        g, u, dr = gate_up(xr, wg, wu, wider, 0, hidden // wider, hidden // wider, Exchange(groups, [('block', dp, 0)], 1))
        arrays = dict(scal=scal, meta=meta_r, x=xr, dy=dr, wd=wd, g=g, u=u)
        for k in own:
            arrays[k + '_own'], arrays[k + '_hot'] = own[k], hot[k]
        cfg = dict(tile=tile, rank=rank, n_local=n_local, scale=scale, groups=groups, cap=cap)
        res_a = mid(arrays, dict(cfg, first=True, last=False, start=0, steps=head))
        n_a, n_b = 2 * head, 2 * (tiles - head)
        for k in ('pg', 'pu', 'qd', 'sel', 'left', 'pd_acc', 'qg_acc', 'qu_acc', 'out_acc', 'gbg', 'gbu', 'gad', 'dg', 'du'):
            arrays[k + '_in'] = res_a[k]
        res_b = mid(arrays, dict(cfg, first=False, last=True, start=head, steps=tiles - head), Exchange(
            groups, [('some', res_a['rows'], n_a), ('all', res_a['prow'], 0), ('block', res_a['drow'], 0)], 2))
        rows_a, early, drow = res_b['x_dst0'], res_b['x_dst1'], res_b['x_dst2']
        gather = lambda v: lax.all_gather(v, 'data', axis=0, tiled=True)
        more_a = gather(slices(scal, rows_a, early, [], rank, n_local, n_a, scale))
        dt = 256
        nd = width // dt // 2
        dx_args = (dr, res_b['qg'], res_b['qu'], own['ag'], hot['ag'], own['au'], hot['au'], res_b['dg'], res_b['du'], wg, wu, dt)
        dxa, rows_b, late = dx_part(*dx_args, 0, nd, Exchange(groups, [('some', res_b['rows'], n_b), ('all', res_b['prow'], 0)], 3))
        more_b = gather(slices(scal, rows_b, early, [late, drow], rank, n_local, n_b, scale))
        dxb, dxa_r, out_r = dx_part(*dx_args, nd, nd, Exchange(groups, [('block', dxa, 0), ('block', res_b['out'], 0)], 4))
        dxb_r, = exchange_only(Exchange(groups, [('block', dxb, 0)], 5))
        out, dx = back(pt, out_r, dxa_r, dxb_r)
        sums = [res_b[k] for k in ('gbg', 'gbu', 'gad', 'gag', 'gau', 'gbd')]
        gbg, gbu, gad, gag, gau, gbd = add_if(
            flag, sums, more_a, more_b, half, tile // 2, width // groups, n_a, n_b, groups)

        far = early[:, 3 * rank + 1]
        agree = jnp.all(((hot_all == hot_f) & (low_all == hot_f)) | (hot_all < 0))
        source = lax.div(jnp.arange(tokens), tokens // groups).astype(F32)
        knows = (hot_f < 0) | jnp.any((source == hot_f) & (hot_all == hot_f))
        ok = agree & knows & jnp.all(far.astype(F32) <= cap)
        fast = (out, dx, gag, gbg, gau, gbu, gad, gbd)

        back_tall = lambda a: jnp.transpose(a.reshape(n_local, rank, a.shape[1]), (0, 2, 1))
        back_flat = lambda a: a.reshape(n_local, rank, a.shape[1])

        def final(out, dx, gag, gbg, gau, gbu, gad, gbd):
            return out, dx, back_tall(gag), back_flat(gbg), back_tall(gau), back_flat(gbu), back_tall(gad), back_flat(gbd)

        def again(carry):
            names = ('ag', 'bg', 'au', 'bu', 'ad', 'bd')
            return (jnp.bool_(False), *final(*ring_path(x, ids, dy, wg, wu, wd, *(own[k] for k in names), groups, n_local, scale)))

        redo = jnp.bool_(True) if force_ring else jnp.logical_not(ok)
        return lax.while_loop(lambda c: c[0], again, (redo, *final(*fast)))[1:]

    return jax.shard_map(
        device_fn,
        mesh=mesh,
        in_specs=(tok_spec, P(('rep', 'data')), tok_spec) + (P(None, None),) * 3 + (own_spec,) * 6,
        out_specs=(tok_spec, tok_spec) + (grad_spec,) * 6,
        check_vma=False,
    )
```

time: 3320 us -> 481 us (0.14)
  blocking collectives: 1180 us -> 0 us
  local copies, waits for them, and re-layouts: 678 us -> 1.95 us
  waiting for transfers between devices: 486 us -> 8.44 us
  matrix products: 311 us -> 0 us
  other arithmetic: 306 us -> 12.5 us
  Pallas kernels: 265 us -> 436 us
  starting transfers between devices: 75.5 us -> 0.37 us
    all_to_all x5 -> x0, blocking collectives: 1180 us -> none  [the longest x3 648 us: to_owner(): arrived = lax.all_to_all(pack_rows(in_rows), 'data', 0, 0, tiled=True)]
    gather x23 -> x0, local copies, waits for them, and re-layouts: 635 us -> none  [the longest x5 204 us: to_source(): jnp.take(owner_rows, restore, axis=0)]
    all_to_all x6 -> x0, waiting for transfers between devices: 486 us -> none  [the longest x3 308 us: to_source(): lax.all_to_all(jnp.take(owner_rows, restore, axis=0), 'data', 0, 0, tiled...]
    pallas_call x0 -> x12, Pallas kernels: none -> 436 us  [the longest x2 122 us: dx_part(): pl.pallas_call(functools.partial(dx_kernel, xchg=xchg, steps=steps), grid...]
    dot_general x6 -> x0, matrix products: 311 us -> none  [the longest x3 164 us: contract_last(): lax.dot_general(left_rows, weight, (((1,), (1,)), ((), ())), preferred_el...]
    another operation x12 -> x0, Pallas kernels: 175 us -> none
    select_n x10 -> x4, other arithmetic: 159 us -> 5.74 us  [device_fn(): jnp.where(i_am_hot, v, jnp.zeros_like(v))]
    convert_element_type x11 -> x0, other arithmetic: 101 us -> none  [the longest x1 23.5 us: device_fn(): (array_b10 * grouped_rows(p_up, b_up, group_sizes, 1)).astype(jnp.bfloat16)]
  transfers between devices with their start and end apart: 6 -> 3, of which waited for: 4 -> 1; matrix products, arithmetic and copies ran while one was open for 9% -> 1% of each run, Pallas kernels for 2% -> 61%
where the time goes in v1:
time: 481 us; the launch traced here: 478 us
  Pallas kernels  436 us (91%)
  between operations  18.8 us (4%)
  other arithmetic  12.5 us (3%)
  waiting for transfers between devices  8.44 us (2%)
    pallas_call x2, Pallas kernels, dx_part(): pl.pallas_call(functools.partial(dx_kernel, xchg=xchg, steps=steps), grid...  122 us
    pallas_call x2, Pallas kernels, mid(): pl.pallas_call(functools.partial(mid_kernel, names=names, cfg=cfg, xchg=x...  118 us
    pallas_call x1, Pallas kernels, gate_up(): pl.pallas_call(functools.partial(gu_kernel, xchg=xchg, steps=steps, old=l...  92.2 us
    pallas_call x2, Pallas kernels, exchange_only(): pl.pallas_call(functools.partial(exchange_kernel, xchg=xchg), in_specs=xc...  70.5 us
    pallas_call x1, Pallas kernels, add_if(): pl.pallas_call(functools.partial(add_kernel, half=half, heads=steps_a), g...  15.4 us
  transfers between devices with their start and end apart: 3, of which 1 were waited for; matrix products, arithmetic and copies ran while one was open for 1% of the time, Pallas kernels for 61%

profile of v1, /device:TPU:97, one launch (start us, length us, event | category | flops | bytes accessed | tf_op | source)
XLA Modules:
  0.0 477.6 jit_solution(5015601417930461610)
XLA Ops:
  7.3 1.4 compare_select_fusion.9
  8.6 5.2 %route.1 = (bf16[256,4096]{1,0:T(8,128)(2,1)}, bf16[256,4096]{1,0:T(8,128)(2,1)}, f32[256,128]{1,0:T(8,128)}, bf16[256,256]{1,0:T(8,128)(2,1)}) custom-call(s32[1,256]{1,0:T(1,128)} %bitcast.88, s32[1,256]{1,0:T(1,128)} %bitcast.87, bf16[256,4096]{1,0:T(8,128)(2,1)} %x_ref.1, bf16[256,4096]{1,0:T(8,128)(2,1)} %d_ref.1), custom_call_target="tpu_custom_call" | custom-call | flops 1073741824 | bytes 8388608 | tf_op jit(solution)/shard_map/route/pallas_call | solution.py:180
  13.8 1.3 fusion.16
  16.5 1.5 broadcast_select_fusion.8
  18.0 0.9 broadcast_select_fusion.11
  19.4 2.3 broadcast_select_fusion.6
  21.7 1.1 broadcast_select_fusion.9
  23.1 49.2 %exchange.2 = (bf16[256,4096]{1,0:T(8,128)(2,1)}, f32[256,128]{1,0:T(8,128)}) custom-call(bf16[256,4096]{1,0:T(8,128)(2,1)} %get-tuple-element.990.refs_0_, f32[256,128]{1,0:T(8,128)} %get-tuple-element.991.refs_1_), custom_call_target="tpu_custom_call" | custom-call | flops 10000000000 | bytes 10000000 | tf_op jit(solution)/shard_map/exchange/pallas_call | solution.py:122
  72.3 1.7 slice_reduce_fusion
  74.7 0.6 pad_add_fusion.refs_0_.scal_ref
  75.3 92.2 %gate_up.1 = (f32[256,14336]{1,0:T(8,128)}, f32[256,14336]{1,0:T(8,128)}, bf16[256,4096]{1,0:T(8,128)(2,1)}) custom-call(bf16[256,4096]{1,0:T(8,128)(2,1)} %get-tuple-element.993.x_ref.refs_2_, bf16[4096,14336]{1,0:T(8,128)(2,1)} %wg_ref.5, bf16[4096,14336]{1,0:T(8,128)(2,1)} %wu_ref.5, bf16[256,4096]{1,0:T(8,128)(2,1)} %get-tuple-element.994.refs_0_), custom_call_target="tpu_custom_call" | custom-call | flops 60129542144 | bytes 264241152 | tf_op jit(solution)/shard_map/gate_up/pallas_call | solution.py:237
  167.5 8.3 %all-reduce.3.cloned.1.call-done = (bf16[64,4096]{1,0:T(8,128)(2,1)}, bf16[64,4096]{1,0:T(8,128)(2,1)}, bf16[64,4096]{1,0:T(8,128)(2,1)}, bf16[64,14336]{1,0:T(8...) async-done(((bf16[64,4096]{1,0:T(8,128)(2,1)}, bf16[64,4096]{1,0:T(8,128)(2,1)}, bf16[64,4096]{1,0:T(8,128)(2,1)}, bf16[64,14336]{1,0:T(8,128)(2,1)}, ...) | async-done | bytes 7077904 | tf_op jit(solution)/shard_map/psum | solution.py:681
  175.8 61.8 %mid.2 = (f32[64,14336]{1,0:T(8,128)}, f32[64,14336]{1,0:T(8,128)}, f32[64,14336]{1,0:T(8,128)}, bf16[256,14336]{1,0:T(8,128)(2,1)}, bf16[256,14336]{1,0:T(8,128...) custom-call(s32[2]{0:T(128)} %pad_add_fusion.refs_0_.scal_ref, ...), custom_call_target="tpu_custom_call" | custom-call | flops 34359738368 | bytes 67108864 | tf_op jit(solution)/shard_map/mid/pallas_call | solution.py:437
  237.6 56.7 %mid.3 = (f32[64,14336]{1,0:T(8,128)}, f32[64,14336]{1,0:T(8,128)}, f32[64,14336]{1,0:T(8,128)}, bf16[256,14336]{1,0:T(8,128)(2,1)}, bf16[256,14336]{1,0:T(8,128...) custom-call(s32[2]{0:T(128)} %pad_add_fusion.refs_0_.scal_ref, ...), custom_call_target="tpu_custom_call", output_to_operand_aliasing={{0}: (24, {}), {1}: (25, {}), {2}: (26, {}), {3}: (27, {}),... | custom-call | flops 25769803776 | bytes 50331648 | tf_op jit(solution)/shard_map/mid/pallas_call | solution.py:437
  294.3 3.0 slices.2
  297.5 52.1 %dx.2 = (bf16[256,2048]{1,0:T(8,128)(2,1)}, bf16[768,768]{1,0:T(8,128)(2,1)}, bf16[768,128]{1,0:T(8,128)(2,1)}) custom-call(bf16[256,4096]{1,0:T(8,128)(2,1)} %get-tuple-element.995.refs_3_.dy_ref, bf16[256,128]{1,0:T(8,128)(2,1)} %get-tuple-element.1017.qg_ref, bf16[256,128]{1,0:T(8,128)(2,1)} %get-tuple-element.1018.qu_ref, bf16[64,4096]{1,0:T(8,128)(2,1)S(1)} %bitcast.79, ...), custom_call_target="tpu_custom_call" | custom-call | flops 30064771072 | bytes 117440512 | tf_op jit(solution)/shard_map/dx/pallas_call | solution.py:478
  349.6 3.5 slices.3
  353.9 1.0 fusion.14
  354.9 1.3 and_reduce_fusion
  357.5 0.8 fusion.13
  359.0 70.2 %dx.3 = (bf16[256,2048]{1,0:T(8,128)(2,1)}, bf16[256,2048]{1,0:T(8,128)(2,1)}, bf16[256,4096]{1,0:T(8,128)(2,1)}) custom-call(bf16[256,4096]{1,0:T(8,128)(2,1)} %get-tuple-element.995.refs_3_.dy_ref, bf16[256,128]{1,0:T(8,128)(2,1)} %get-tuple-element.1017.qg_ref, bf16[256,128]{1,0:T(8,128)(2,1)} %get-tuple-element.1018.qu_ref, ...), custom_call_target="tpu_custom_call" | custom-call | flops 30064771072 | bytes 117440512 | tf_op jit(solution)/shard_map/dx/pallas_call | solution.py:478
  429.1 21.3 %exchange.3.dxb_in = bf16[256,2048]{1,0:T(8,128)(2,1)} custom-call(bf16[256,2048]{1,0:T(8,128)(2,1)} %get-tuple-element.1027.refs_0_), custom_call_target="tpu_custom_call" | custom-call | flops 10000000000 | bytes 10000000 | tf_op jit(solution)/shard_map/exchange/pallas_call | solution.py:122
  450.5 4.9 %back.1 = (bf16[256,4096]{1,0:T(8,128)(2,1)}, bf16[256,4096]{1,0:T(8,128)(2,1)}) custom-call(bf16[256,256]{1,0:T(8,128)(2,1)} %get-tuple-element.1016.pt_ref, bf16[256,4096]{1,0:T(8,128)(2,1)} %get-tuple-element.1025.out_in, bf16[256,2048]{1,0:T(8,128)(2,1)} %get-tuple-element.1026.dxa_in, bf16[256,2048]{1,0:T(8,128)(2,1)} %exchange.3.dxb_in), custom_call_target="tpu_custom_call" | custom-call | flops 1073741824 | bytes 8388608 | tf_op jit(solution)/shard_map/back/pallas_call | solution.py:204
  455.4 15.4 %add_if.1 = (f32[64,14336]{1,0:T(8,128)}, f32[64,14336]{1,0:T(8,128)}, f32[64,14336]{1,0:T(8,128)}, f32[64,4096]{1,0:T(8,128)}, f32[64,4096]{1,0:T(8,128)}, /*index=5*/f32[64,4096]{1,0:T(8,128)}) custom-call(s32[1]{0:T(128)} %bitcast.30.flag_ref, f32[64,14336]{1,0:T(8,128)} %get-tuple-element.1030.refs_0_, f32[64,14336]{1,0:T(8,128)} %get-tuple-element.1031.refs_1_, ...), custom_call_target="tpu_custom_call" | custom-call | tf_op jit(solution)/shard_map/add_if/pallas_call | solution.py:561
  (33 shorter events, 1.1 us)
Async XLA Ops:
  7.2 9.3 %copy-start.30 = (bf16[2,32,14336]{2,1,0:T(8,128)(2,1)S(1)}, bf16[2,32,14336]{2,1,0:T(8,128)(2,1)}, u32[]{:S(2)}) copy-start(bf16[2,32,14336]{2,1,0:T(8,128)(2,1)} %param.25) | copy-start | bytes 5505028
  7.2 168.6 %all-reduce.3.cloned.1.call-start = ((), (), s32[]{:S(2)}) async-start(), calls=%async_computation.2 | async-start | bytes 14155776 | tf_op jit(solution)/shard_map/psum | solution.py:681
  13.8 4.2 copy-start.43
  16.5 2.4 copy-start.33
  16.5 2.9 copy-start.35
  19.4 2.3 copy-start.37
  19.4 2.3 copy-start.40
  22.9 432.5 %all-gather.3.cloned.1.call-start = ((), (), s32[]{:S(2)}) async-start(), calls=%async_computation | async-start | bytes 6488064 | tf_op jit(solution)/shard_map/all_gather | solution.py:704
  294.3 3.2 copy-start.38
  294.3 3.2 copy-start.41
  297.4 158.0 %all-gather.5.cloned.1.call-start = ((), (), s32[]{:S(2)}) async-start(), calls=%async_computation.1 | async-start | bytes 9732096 | tf_op jit(solution)/shard_map/all_gather | solution.py:704
  349.6 4.3 copy-start.45
  349.6 7.9 %copy-start.47 = (bf16[768,128]{1,0:T(8,128)(2,1)S(1)}, bf16[768,128]{1,0:T(8,128)(2,1)}, u32[]{:S(2)}) copy-start(bf16[768,128]{1,0:T(8,128)(2,1)} %get-tuple-element.1015.early_ref) | copy-start | bytes 589828
  455.4 15.4 %copy-start.31 = (bf16[2,32,14336]{2,1,0:T(8,128)(2,1)S(1)}, bf16[2,32,14336]{2,1,0:T(8,128)(2,1)}, u32[]{:S(2)}) copy-start(bf16[2,32,14336]{2,1,0:T(8,128)(2,1)} %param.25) | copy-start | bytes 5505028
  455.4 15.4 %copy-start.46 = (s32[256]{0:T(256)S(1)}, s32[256]{0:T(256)}, u32[]{:S(2)}) copy-start(s32[256]{0:T(256)} %param.19) | copy-start | bytes 3076
Sparse Core Ops, SparseCore 0:
  23.0 152.7 all-reduce.2
  297.5 53.7 all-gather.2
  354.0 74.8 all-gather.4
